TPU v7x, 128 devices: a whole 4x4x4 slice. The times are simulated.
128 devices in a mesh: gx: 8 (over x_lo, y), gy: 16 (over x_hi, z, core).
Axes of the slice: x: 4 (x_hi: 2, x_lo: 2; x = x_hi * 2 + x_lo), y: 4, z: 4, core: 2. Of those that a mesh axis runs over, the one named last changes fastest.
Arguments:
- density: float32 [64, 64, 128], P('gx', 'gy'), may hold values from -5 to 5
- susceptibility: float32 [64, 64, 128], P('gx', 'gy'), may hold values from -5 to 5
- station_cell: int32 [2, 2048], P(None, 'gx'), may hold values from 0 to 4095
- station_line: int32 [2, 2048], P(None, 'gx'), may hold values from 0 to 255, as said below
- observed: float32 [2, 2048], P(None, 'gx'), may hold values from -3 to 3
- data_weight: float32 [2, 2048], P(None, 'gx'), may hold values from 0.5 to 2
- trial_steps: float32 [8], replicated, may hold values from 0.05 to 0.5
Outputs:
- data_gradient: float32 [2, 64, 64, 128], P(None, 'gx', 'gy')
- cross_force: float32 [2, 64, 64, 128], P(None, 'gx', 'gy')
- weighted_residual: float32 [2, 2048], P(None, 'gx')
- trial_values: float32 [8], replicated
Inputs may be any that keep to these rules, and one draw needn't show every extreme that they name: `station_line`: one or more survey lines hold no station of either field.
All inputs are finite; a program needn't handle non-finite values. Where the computation divides by a largest or mean magnitude, that divisor is 1e-20 or more.
Results may differ from a plain program's by a relative error of at most 0.0003.
Values sent between devices are 32-bit elements; how exact they have to be, the bound alone decides.
A program may use at most 64 MiB of HBM per device.

v0:
```python
import math

import jax
import jax.numpy as jnp
from jax import lax
from jax.sharding import Mesh
from jax.sharding import PartitionSpec as P

LINES = 256
GX = ("gx_0", "gx_1")
GX_GY = ("gx_0", "gx_1", "gy_0", "gy_1", "gy_2")
GY = ("gy_0", "gy_1", "gy_2")


cell_depth = 2.0
lift = 1.0
coupling_scale = 0.05
highest = lax.Precision.HIGHEST


def from_everyone(value, axis):
    copies = jnp.broadcast_to(value, (lax.axis_size(axis), *value.shape))
    return lax.all_to_all(copies, axis, split_axis=0, concat_axis=0, tiled=True)


def over_copies(value, axis):
    return from_everyone(value, axis).sum(axis=0)


def extended_2(block, sides, width):
    for axis, dim in sides:
        count = lax.axis_size(axis)
        forward = [(i, i + 1) for i in range(count - 1)]
        backward = [(target, source) for source, target in forward]
        low = lax.ppermute(
            lax.slice_in_dim(block, block.shape[dim] - width, None, axis=dim), axis, forward
        )
        high = lax.ppermute(lax.slice_in_dim(block, 0, width, axis=dim), axis, backward)
        block = jnp.concatenate([low, block, high], axis=dim)
    return block


def in_order(tiles, dim):
    shape = list(tiles.shape[1:])
    shape[dim] *= tiles.shape[0]
    return jnp.moveaxis(tiles, 0, dim).reshape(shape)


def gathered_copies(value, axis, dim):
    tiles = from_everyone(value, axis)
    return in_order(tiles, dim)


def in_blocks(value, dim, devices):
    shape = value.shape
    tiles = value.reshape(*shape[:dim], devices, shape[dim] // devices, *shape[dim + 1 :])
    return jnp.moveaxis(tiles, dim, 0)


def sent_and_summed(value, axis, dim):
    devices = lax.axis_size(axis)
    tiles = lax.all_to_all(in_blocks(value, dim, devices), axis, 0, 0, tiled=True)
    return jnp.sum(tiles, axis=0)


def over_axes(value, axes):
    for axis in axes:
        value = lax.pmax(value, axis)
    return value


def over_axes_2(value, axes):
    for axis in axes:
        value = lax.psum(value, axis)
    return value


def kernel_tile(field, station_x, station_y, cell_x, cell_y, depth):
    gap_x = station_x[:, None] - cell_x[None, :]
    gap_y = station_y[:, None] - cell_y[None, :]
    depth_row = depth[None, :]
    radius_sq = gap_x * gap_x + gap_y * gap_y + depth_row * depth_row
    inverse = lax.rsqrt(radius_sq)
    cube = inverse * inverse * inverse
    if field == 0:
        return depth_row * cube
    return (3.0 * depth_row * depth_row - radius_sq) * cube * inverse * inverse


def cell_coords(anchor_x, anchor_y, width, layers, start, count):
    position = start + jnp.arange(count, dtype=jnp.int32)
    cell_x = (anchor_x + position // (width * layers)).astype(jnp.float32)
    cell_y = (anchor_y + position // layers % width).astype(jnp.float32)
    depth = ((position % layers).astype(jnp.float32) + 0.5) * cell_depth + lift
    return (cell_x, cell_y, depth)


def to_blocks(values, size):
    return jnp.swapaxes(values.reshape(2, -1, size), 0, 1)


def forward_part(models, anchor_x, anchor_y, station_x, station_y):
    rows, width, layers = (models.shape[1], models.shape[2], models.shape[3])
    cells = rows * width * layers
    flat = models.reshape(2, cells)
    cell_block = math.gcd(cells, 2048)
    station_block = math.gcd(station_x.shape[1], 64)

    def forward_station_turn(pair):
        block_x, block_y = pair

        def forward_cell_turn(index, total):
            start = index * cell_block
            cell_x, cell_y, depth = cell_coords(
                anchor_x, anchor_y, width, layers, start, cell_block
            )
            piece = lax.dynamic_slice_in_dim(flat, start, cell_block, 1)
            rows_out = [
                jnp.dot(
                    kernel_tile(field, block_x[field], block_y[field], cell_x, cell_y, depth),
                    piece[field],
                    precision=highest,
                )
                for field in range(2)
            ]
            return total + jnp.stack(rows_out)

        return lax.fori_loop(
            0, cells // cell_block, forward_cell_turn, jnp.zeros((2, station_block), jnp.float32)
        )

    parts = lax.map(
        forward_station_turn,
        (to_blocks(station_x, station_block), to_blocks(station_y, station_block)),
    )
    return jnp.swapaxes(parts, 0, 1).reshape(2, -1)


def adjoint_part(source, anchor_x, anchor_y, rows, width, layers, station_x, station_y):
    cells = rows * width * layers
    cell_block = math.gcd(cells, 2048)
    station_block = math.gcd(station_x.shape[1], 64)

    def adjoint_cell_turn(index):
        start = index * cell_block
        cell_x, cell_y, depth = cell_coords(anchor_x, anchor_y, width, layers, start, cell_block)

        def cell_station_turn(turn, total):
            first = turn * station_block
            block_x = lax.dynamic_slice_in_dim(station_x, first, station_block, 1)
            block_y = lax.dynamic_slice_in_dim(station_y, first, station_block, 1)
            block_source = lax.dynamic_slice_in_dim(source, first, station_block, 1)
            rows_out = [
                jnp.dot(
                    block_source[field],
                    kernel_tile(field, block_x[field], block_y[field], cell_x, cell_y, depth),
                    precision=highest,
                )
                for field in range(2)
            ]
            return total + jnp.stack(rows_out)

        return lax.fori_loop(
            0,
            station_x.shape[1] // station_block,
            cell_station_turn,
            jnp.zeros((2, cell_block), jnp.float32),
        )

    parts = lax.map(adjoint_cell_turn, jnp.arange(cells // cell_block, dtype=jnp.int32))
    return jnp.swapaxes(parts, 0, 1).reshape(2, rows, width, layers)


def cross_terms(extended, start_x, start_y, total_x, total_y):
    rows = extended.shape[1] - 1
    width = extended.shape[2] - 1
    global_x = start_x - 1 + jnp.arange(rows, dtype=jnp.int32)
    global_y = start_y - 1 + jnp.arange(width, dtype=jnp.int32)
    mask_x = (global_x < total_x - 1).astype(jnp.float32)[:, None, None]
    mask_y = (global_y < total_y - 1).astype(jnp.float32)[None, :, None]
    valid = ((global_x >= 0)[:, None] & (global_y >= 0)[None, :]).astype(jnp.float32)[:, :, None]

    def diffs(field):
        base = field[:-1, :-1, :]
        along_x = (field[1:, :-1, :] - base) * mask_x
        along_y = (field[:-1, 1:, :] - base) * mask_y
        along_z = jnp.concatenate(
            [base[:, :, 1:] - base[:, :, :-1], jnp.zeros_like(base[:, :, :1])], axis=2
        )
        return (along_x, along_y, along_z)

    first_x, first_y, first_z = diffs(extended[0])
    second_x, second_y, second_z = diffs(extended[1])
    part_one = first_y * second_z - first_z * second_y
    part_two = first_z * second_x - first_x * second_z
    part_three = first_x * second_y - first_y * second_x
    return (part_one * part_one + part_two * part_two + part_three * part_three) * valid


def line_totals(values, lines):
    labels = jnp.arange(LINES, dtype=jnp.int32)
    onehot = (lines[:, :, None] == labels).astype(jnp.float32)
    local = jnp.einsum("fs,fsl->fl", values, onehot, precision=highest)
    return over_copies(local, GX)


def spread_table(table, lines):
    labels = jnp.arange(LINES, dtype=jnp.int32)
    onehot = (lines[:, :, None] == labels).astype(jnp.float32)
    return jnp.einsum("fl,fsl->fs", table, onehot, precision=highest)


def faces(fields):
    return extended_2(fields, ((GX, 1), (GY, 2)), 1)


def body(density, susceptibility, station_cell, station_line, observed, data_weight, trial_steps):
    rows, width, layers = density.shape
    groups = lax.axis_size(GX)
    columns = lax.axis_size(GY)
    total_x = rows * groups
    total_y = width * columns
    own_count = station_cell.shape[1]
    total_stations = own_count * groups
    anchor_x = lax.axis_index(GX) * rows
    anchor_y = lax.axis_index(GY) * width
    models = jnp.stack([density, susceptibility])
    own_x = (station_cell // total_y).astype(jnp.float32)
    own_y = (station_cell % total_y).astype(jnp.float32)
    coupling = coupling_scale * total_stations / (total_x * total_y * layers)

    def energies(extended):
        squares = cross_terms(extended, anchor_x, anchor_y, total_x, total_y)
        return (0.5 * jnp.sum(squares), 0.5 * jnp.sum(squares[1:, 1:]))

    extended = faces(models)
    (rim_energy, model_energy), rim_grad = jax.value_and_grad(energies, has_aux=True)(extended)
    cross_force = rim_grad[:, 1:-1, 1:-1, :]

    def fold_forward(piece, start):
        return forward_part(piece, start, anchor_y, own_x, own_y)

    def column_data(fields):
        partial_value = fold_forward(gathered_copies(fields, GX, 1), jnp.int32(0))
        return over_copies(partial_value, GY)

    predicted = column_data(models)
    misfit = predicted - observed
    both_lines = jnp.concatenate([station_line, station_line])
    first_totals = line_totals(jnp.concatenate([misfit, jnp.ones_like(misfit)]), both_lines)
    counts = jnp.maximum(first_totals[2:], 1.0)
    residual = misfit - spread_table(first_totals[:2] / counts, station_line)
    weighted_residual = data_weight * residual
    source = data_weight * weighted_residual
    source = source - spread_table(line_totals(source, station_line) / counts, station_line)
    data_gradient = jnp.swapaxes(
        sent_and_summed(
            jnp.swapaxes(
                adjoint_part(
                    source,
                    jnp.int32(0),
                    anchor_y,
                    rows * lax.axis_size(GX),
                    width,
                    layers,
                    own_x,
                    own_y,
                ),
                0,
                1,
            ),
            GX,
            0,
        ),
        0,
        1,
    )
    gradient = data_gradient + coupling * cross_force
    peak = over_axes(jnp.max(jnp.abs(gradient)), GX_GY) + 1e-06
    direction = gradient / peak
    extended_direction = faces(direction)
    image = column_data(direction)
    change = image - spread_table(line_totals(image, station_line) / counts, station_line)
    shares = []
    for trial in range(trial_steps.shape[0]):
        step = trial_steps[trial]
        moved = data_weight * (residual - step * change)
        data_value = 0.5 * jnp.sum(moved * moved)
        own_extended = extended - step * extended_direction
        shares.append(
            data_value / columns
            + coupling
            * (
                0.5
                * jnp.sum(cross_terms(own_extended, anchor_x, anchor_y, total_x, total_y)[1:, 1:])
            )
        )
    trial_values = over_axes_2(jnp.stack(shares), GX_GY) / (2 * total_stations)
    return (data_gradient, cross_force, weighted_residual, trial_values)


def solution(mesh):
    torus = Mesh(mesh.devices.reshape(2, 4, 2, 4, 2), ("gx_0", "gx_1", "gy_0", "gy_1", "gy_2"))
    in_specs = (
        P(GX, GY, None),
        P(GX, GY, None),
        P(None, GX),
        P(None, GX),
        P(None, GX),
        P(None, GX),
        P(),
    )
    out_specs = (P(None, GX, GY, None), P(None, GX, GY, None), P(None, GX), P())
    return jax.shard_map(body, mesh=torus, in_specs=in_specs, out_specs=out_specs, check_vma=False)
```

profile of v0, /device:TPU:1, one launch (start us, length us, event | category | flops | bytes accessed | tf_op | source)
XLA Modules:
  0.0 549.9 jit_solution(10390206426090094262)
XLA Ops:
  1.4 4.0 collective-permute-start
  5.4 1.3 collective-permute-start.1
  7.5 5.9 %all-to-all-start = ((f32[8,2,8,4,128]{4,3,2,1,0:T(4,128)}), f32[8,2,8,4,128]{4,3,2,1,0:T(4,128)S(1)}, u32[]{:S(2)}, u32[]{:S(2)}) async-start(f32[8,2,8,4,128]{4,3,2,1,0:T(4,128)} %broadcast_in_dim.85), calls=%async_computation | async-start | bytes 524288 | tf_op jit(solution)/shard_map/all_to_all | solution.py:23
  14.2 4.9 collective-permute-start.2
  19.2 1.9 collective-permute-start.3
  21.3 2.8 collective-permute-done.3
  24.7 106.4 %while.116 = (s32[]{:T(128)}, f32[4,2,64]{2,1,0:T(2,128)S(1)}, f32[4,2,64]{2,1,0:T(2,128)S(1)}, f32[4,2,64]{2,1,0:T(2,128)S(1)}, s32[]{:T(128)}, /*index=5*/f32[...) while((s32[]{:T(128)}, f32[4,2,64]{2,1,0:T(2,128)S(1)}, ...), condition=%wide.region_3.4_spmd, body=%wide.region_0.3_spmd.sunk | while | flops 6052234 | bytes 133554 | solution.py:132
  24.7 26.5 %while.121 = (s32[]{:T(128)}, f32[2,64]{1,0:T(2,128)S(1)}, f32[2,64]{1,0:T(2,128)S(1)}, f32[2,64]{1,0:T(2,128)S(1)}, s32[]{:T(128)}, /*index=5*/f32[2,32768]{1,0...) while((s32[]{:T(128)}, f32[2,64]{1,0:T(2,128)S(1)}, ...), condition=%wide.region_2.2_spmd.clone, body=%wide.region_1.1_spmd.clone.sunk | while | flops 6052232 | bytes 129229 | solution.py:128
  25.5 0.8 fusion.268
  27.2 0.8 fusion.268
  28.9 0.8 fusion.268
  51.3 26.5 %while.121 = (s32[]{:T(128)}, f32[2,64]{1,0:T(2,128)S(1)}, f32[2,64]{1,0:T(2,128)S(1)}, f32[2,64]{1,0:T(2,128)S(1)}, s32[]{:T(128)}, /*index=5*/f32[2,32768]{1,0...) while((s32[]{:T(128)}, f32[2,64]{1,0:T(2,128)S(1)}, ...), condition=%wide.region_2.2_spmd.clone, body=%wide.region_1.1_spmd.clone.sunk | while | flops 6052232 | bytes 129229 | solution.py:128
  77.9 26.5 %while.121 = (s32[]{:T(128)}, f32[2,64]{1,0:T(2,128)S(1)}, f32[2,64]{1,0:T(2,128)S(1)}, f32[2,64]{1,0:T(2,128)S(1)}, s32[]{:T(128)}, /*index=5*/f32[2,32768]{1,0...) while((s32[]{:T(128)}, f32[2,64]{1,0:T(2,128)S(1)}, ...), condition=%wide.region_2.2_spmd.clone, body=%wide.region_1.1_spmd.clone.sunk | while | flops 6052232 | bytes 129229 | solution.py:128
  104.5 26.5 %while.121 = (s32[]{:T(128)}, f32[2,64]{1,0:T(2,128)S(1)}, f32[2,64]{1,0:T(2,128)S(1)}, f32[2,64]{1,0:T(2,128)S(1)}, s32[]{:T(128)}, /*index=5*/f32[2,32768]{1,0...) while((s32[]{:T(128)}, f32[2,64]{1,0:T(2,128)S(1)}, ...), condition=%wide.region_2.2_spmd.clone, body=%wide.region_1.1_spmd.clone.sunk | while | flops 6052232 | bytes 129229 | solution.py:128
  131.8 8.5 %all-to-all-start.1 = ((f32[16,2,256]{2,1,0:T(2,128)}), f32[16,2,256]{2,1,0:T(2,128)S(1)}, u32[]{:S(2)}, u32[]{:S(2)}) async-start(f32[16,2,256]{2,1,0:T(2,128)} %broadcast_in_dim.86), calls=%async_computation.1 | async-start | bytes 65536 | tf_op jit(solution)/shard_map/all_to_all | solution.py:23
  140.4 7.3 %all-to-all-done.1 = f32[16,2,256]{2,1,0:T(2,128)S(1)} async-done(((f32[16,2,256]{2,1,0:T(2,128)}), f32[16,2,256]{2,1,0:T(2,128)S(1)}, u32[]{:S(2)}, u32[]{:S(2)}) %all-to-all-start.1) | async-done | bytes 32800 | tf_op jit(solution)/shard_map/all_to_all | solution.py:23
  148.8 4.8 all-to-all-start.2
  153.7 5.0 all-to-all-done.2
  161.0 3.3 all-to-all-start.3
  164.4 5.0 all-to-all-done.3
  169.8 121.7 %while.118 = (s32[]{:T(128)}, f32[16,2,2048]{2,1,0:T(2,128)S(1)}, s32[16]{0:T(128)S(1)}, s32[]{:T(128)}, f32[2,256]{1,0:T(2,128)S(1)}, /*index=5*/f32[2,256]{1,0...) while((s32[]{:T(128)}, f32[16,2,2048]{2,1,0:T(2,128)S(1)}, ...), condition=%wide.region_10.11_spmd, body=%wide.region_7.10_spmd.sunk | while | flops 6064138 | bytes 213438 | solution.py:170
  171.0 6.3 %while.122 = (s32[]{:T(128)}, f32[2,2048]{1,0:T(2,128)S(1)}, f32[2,256]{1,0:T(2,128)S(1)}, f32[2,256]{1,0:T(2,128)S(1)}, f32[2,256]{1,0:T(2,128)S(1)}, /*index=5...) while((s32[]{:T(128)}, f32[2,2048]{1,0:T(2,128)S(1)}, ...), condition=%wide.region_9.9_spmd.clone.clone.clone, body=%wide.region_8.8_spmd.clone.clone.clone.sunk | while | flops 6064135 | bytes 180413 | solution.py:163
  178.6 6.3 %while.122 = (s32[]{:T(128)}, f32[2,2048]{1,0:T(2,128)S(1)}, f32[2,256]{1,0:T(2,128)S(1)}, f32[2,256]{1,0:T(2,128)S(1)}, f32[2,256]{1,0:T(2,128)S(1)}, /*index=5...) while((s32[]{:T(128)}, f32[2,2048]{1,0:T(2,128)S(1)}, ...), condition=%wide.region_9.9_spmd.clone.clone.clone, body=%wide.region_8.8_spmd.clone.clone.clone.sunk | while | flops 6064135 | bytes 180413 | solution.py:163
  186.2 6.3 %while.122 = (s32[]{:T(128)}, f32[2,2048]{1,0:T(2,128)S(1)}, f32[2,256]{1,0:T(2,128)S(1)}, f32[2,256]{1,0:T(2,128)S(1)}, f32[2,256]{1,0:T(2,128)S(1)}, /*index=5...) while((s32[]{:T(128)}, f32[2,2048]{1,0:T(2,128)S(1)}, ...), condition=%wide.region_9.9_spmd.clone.clone.clone, body=%wide.region_8.8_spmd.clone.clone.clone.sunk | while | flops 6064135 | bytes 180413 | solution.py:163
  193.8 6.3 %while.122 = (s32[]{:T(128)}, f32[2,2048]{1,0:T(2,128)S(1)}, f32[2,256]{1,0:T(2,128)S(1)}, f32[2,256]{1,0:T(2,128)S(1)}, f32[2,256]{1,0:T(2,128)S(1)}, /*index=5...) while((s32[]{:T(128)}, f32[2,2048]{1,0:T(2,128)S(1)}, ...), condition=%wide.region_9.9_spmd.clone.clone.clone, body=%wide.region_8.8_spmd.clone.clone.clone.sunk | while | flops 6064135 | bytes 180413 | solution.py:163
  201.4 6.3 %while.122 = (s32[]{:T(128)}, f32[2,2048]{1,0:T(2,128)S(1)}, f32[2,256]{1,0:T(2,128)S(1)}, f32[2,256]{1,0:T(2,128)S(1)}, f32[2,256]{1,0:T(2,128)S(1)}, /*index=5...) while((s32[]{:T(128)}, f32[2,2048]{1,0:T(2,128)S(1)}, ...), condition=%wide.region_9.9_spmd.clone.clone.clone, body=%wide.region_8.8_spmd.clone.clone.clone.sunk | while | flops 6064135 | bytes 180413 | solution.py:163
  209.1 6.3 %while.122 = (s32[]{:T(128)}, f32[2,2048]{1,0:T(2,128)S(1)}, f32[2,256]{1,0:T(2,128)S(1)}, f32[2,256]{1,0:T(2,128)S(1)}, f32[2,256]{1,0:T(2,128)S(1)}, /*index=5...) while((s32[]{:T(128)}, f32[2,2048]{1,0:T(2,128)S(1)}, ...), condition=%wide.region_9.9_spmd.clone.clone.clone, body=%wide.region_8.8_spmd.clone.clone.clone.sunk | while | flops 6064135 | bytes 180413 | solution.py:163
  216.7 6.3 %while.122 = (s32[]{:T(128)}, f32[2,2048]{1,0:T(2,128)S(1)}, f32[2,256]{1,0:T(2,128)S(1)}, f32[2,256]{1,0:T(2,128)S(1)}, f32[2,256]{1,0:T(2,128)S(1)}, /*index=5...) while((s32[]{:T(128)}, f32[2,2048]{1,0:T(2,128)S(1)}, ...), condition=%wide.region_9.9_spmd.clone.clone.clone, body=%wide.region_8.8_spmd.clone.clone.clone.sunk | while | flops 6064135 | bytes 180413 | solution.py:163
  224.3 6.3 %while.122 = (s32[]{:T(128)}, f32[2,2048]{1,0:T(2,128)S(1)}, f32[2,256]{1,0:T(2,128)S(1)}, f32[2,256]{1,0:T(2,128)S(1)}, f32[2,256]{1,0:T(2,128)S(1)}, /*index=5...) while((s32[]{:T(128)}, f32[2,2048]{1,0:T(2,128)S(1)}, ...), condition=%wide.region_9.9_spmd.clone.clone.clone, body=%wide.region_8.8_spmd.clone.clone.clone.sunk | while | flops 6064135 | bytes 180413 | solution.py:163
  231.9 6.3 %while.122 = (s32[]{:T(128)}, f32[2,2048]{1,0:T(2,128)S(1)}, f32[2,256]{1,0:T(2,128)S(1)}, f32[2,256]{1,0:T(2,128)S(1)}, f32[2,256]{1,0:T(2,128)S(1)}, /*index=5...) while((s32[]{:T(128)}, f32[2,2048]{1,0:T(2,128)S(1)}, ...), condition=%wide.region_9.9_spmd.clone.clone.clone, body=%wide.region_8.8_spmd.clone.clone.clone.sunk | while | flops 6064135 | bytes 180413 | solution.py:163
  239.5 6.3 %while.122 = (s32[]{:T(128)}, f32[2,2048]{1,0:T(2,128)S(1)}, f32[2,256]{1,0:T(2,128)S(1)}, f32[2,256]{1,0:T(2,128)S(1)}, f32[2,256]{1,0:T(2,128)S(1)}, /*index=5...) while((s32[]{:T(128)}, f32[2,2048]{1,0:T(2,128)S(1)}, ...), condition=%wide.region_9.9_spmd.clone.clone.clone, body=%wide.region_8.8_spmd.clone.clone.clone.sunk | while | flops 6064135 | bytes 180413 | solution.py:163
  247.1 6.3 %while.122 = (s32[]{:T(128)}, f32[2,2048]{1,0:T(2,128)S(1)}, f32[2,256]{1,0:T(2,128)S(1)}, f32[2,256]{1,0:T(2,128)S(1)}, f32[2,256]{1,0:T(2,128)S(1)}, /*index=5...) while((s32[]{:T(128)}, f32[2,2048]{1,0:T(2,128)S(1)}, ...), condition=%wide.region_9.9_spmd.clone.clone.clone, body=%wide.region_8.8_spmd.clone.clone.clone.sunk | while | flops 6064135 | bytes 180413 | solution.py:163
  254.7 6.3 %while.122 = (s32[]{:T(128)}, f32[2,2048]{1,0:T(2,128)S(1)}, f32[2,256]{1,0:T(2,128)S(1)}, f32[2,256]{1,0:T(2,128)S(1)}, f32[2,256]{1,0:T(2,128)S(1)}, /*index=5...) while((s32[]{:T(128)}, f32[2,2048]{1,0:T(2,128)S(1)}, ...), condition=%wide.region_9.9_spmd.clone.clone.clone, body=%wide.region_8.8_spmd.clone.clone.clone.sunk | while | flops 6064135 | bytes 180413 | solution.py:163
  262.3 6.3 %while.122 = (s32[]{:T(128)}, f32[2,2048]{1,0:T(2,128)S(1)}, f32[2,256]{1,0:T(2,128)S(1)}, f32[2,256]{1,0:T(2,128)S(1)}, f32[2,256]{1,0:T(2,128)S(1)}, /*index=5...) while((s32[]{:T(128)}, f32[2,2048]{1,0:T(2,128)S(1)}, ...), condition=%wide.region_9.9_spmd.clone.clone.clone, body=%wide.region_8.8_spmd.clone.clone.clone.sunk | while | flops 6064135 | bytes 180413 | solution.py:163
  269.9 6.3 %while.122 = (s32[]{:T(128)}, f32[2,2048]{1,0:T(2,128)S(1)}, f32[2,256]{1,0:T(2,128)S(1)}, f32[2,256]{1,0:T(2,128)S(1)}, f32[2,256]{1,0:T(2,128)S(1)}, /*index=5...) while((s32[]{:T(128)}, f32[2,2048]{1,0:T(2,128)S(1)}, ...), condition=%wide.region_9.9_spmd.clone.clone.clone, body=%wide.region_8.8_spmd.clone.clone.clone.sunk | while | flops 6064135 | bytes 180413 | solution.py:163
  277.5 6.3 %while.122 = (s32[]{:T(128)}, f32[2,2048]{1,0:T(2,128)S(1)}, f32[2,256]{1,0:T(2,128)S(1)}, f32[2,256]{1,0:T(2,128)S(1)}, f32[2,256]{1,0:T(2,128)S(1)}, /*index=5...) while((s32[]{:T(128)}, f32[2,2048]{1,0:T(2,128)S(1)}, ...), condition=%wide.region_9.9_spmd.clone.clone.clone, body=%wide.region_8.8_spmd.clone.clone.clone.sunk | while | flops 6064135 | bytes 180413 | solution.py:163
  285.1 6.3 %while.122 = (s32[]{:T(128)}, f32[2,2048]{1,0:T(2,128)S(1)}, f32[2,256]{1,0:T(2,128)S(1)}, f32[2,256]{1,0:T(2,128)S(1)}, f32[2,256]{1,0:T(2,128)S(1)}, /*index=5...) while((s32[]{:T(128)}, f32[2,2048]{1,0:T(2,128)S(1)}, ...), condition=%wide.region_9.9_spmd.clone.clone.clone, body=%wide.region_8.8_spmd.clone.clone.clone.sunk | while | flops 6064135 | bytes 180413 | solution.py:163
  292.5 3.4 all-to-all-start.4
  296.1 5.9 %all-to-all-done.4 = f32[8,8,2,4,128]{4,3,1,2,0:T(4,128)S(1)} async-done(((f32[8,8,2,4,128]{4,3,1,2,0:T(4,128)}), f32[8,8,2,4,128]{4,3,1,2,0:T(4,128)S(1)}, u32[]{:S(2)}, u32[]{:S(2)}) %all-to-all-start.4) | async-done | bytes 262176 | tf_op jit(solution)/shard_map/all_to_all | solution.py:62
  302.6 4.4 pmax.35
  307.0 7.1 %pmax.36 = f32[]{:T(128)} all-reduce(f32[]{:T(128)} %pmax.35), channel_id=1, replica_groups=mesh['gx_0'=2,'gx_1'=4,'gy_0'=2,'gy_1'=4,'gy_2'=2] {'gx_1'}, use_global_device_ids=true, to_apply=%region_14.15 | all-reduce | flops 1 | bytes 8 | tf_op jit(solution)/shard_map/pmax | solution.py:68
  314.1 5.9 %pmax.37 = f32[]{:T(128)} all-reduce(f32[]{:T(128)} %pmax.36), channel_id=1, replica_groups=mesh['gx_0'=2,'gx_1'=4,'gy_0'=2,'gy_1'=4,'gy_2'=2] {'gy_0'}, use_global_device_ids=true, to_apply=%region_15.16 | all-reduce | flops 1 | bytes 8 | tf_op jit(solution)/shard_map/pmax | solution.py:68
  320.0 7.8 %pmax.38 = f32[]{:T(128)} all-reduce(f32[]{:T(128)} %pmax.37), channel_id=1, replica_groups=mesh['gx_0'=2,'gx_1'=4,'gy_0'=2,'gy_1'=4,'gy_2'=2] {'gy_1'}, use_global_device_ids=true, to_apply=%region_16.17 | all-reduce | flops 1 | bytes 8 | tf_op jit(solution)/shard_map/pmax | solution.py:68
  327.9 12.9 %pmax.39 = f32[]{:T(128)} all-reduce(f32[]{:T(128)} %pmax.38), channel_id=1, replica_groups=mesh['gx_0'=2,'gx_1'=4,'gy_0'=2,'gy_1'=4,'gy_2'=2] {'gy_2'}, use_global_device_ids=true, to_apply=%region_17.18 | all-reduce | flops 1 | bytes 8 | tf_op jit(solution)/shard_map/pmax | solution.py:68
  341.5 2.8 collective-permute-start.4
  344.3 1.3 collective-permute-start.5
  345.7 3.0 collective-permute-done.5
  348.7 4.1 collective-permute-start.6
  352.8 1.9 collective-permute-start.7
  356.2 5.8 %all-to-all-start.5 = ((f32[8,2,8,4,128]{4,3,2,1,0:T(4,128)}), f32[8,2,8,4,128]{4,3,2,1,0:T(4,128)S(1)}, u32[]{:S(2)}, u32[]{:S(2)}) async-start(f32[8,2,8,4,128]{4,3,2,1,0:T(4,128)} %broadcast_in_dim.93), calls=%async_computation.5 | async-start | bytes 524288 | tf_op jit(solution)/shard_map/all_to_all | solution.py:23
  370.5 106.4 %while.120 = (s32[]{:T(128)}, f32[4,2,64]{2,1,0:T(2,128)S(1)}, f32[4,2,64]{2,1,0:T(2,128)S(1)}, f32[4,2,64]{2,1,0:T(2,128)S(1)}, s32[]{:T(128)}, /*index=5*/f32[...) while((s32[]{:T(128)}, f32[4,2,64]{2,1,0:T(2,128)S(1)}, ...), condition=%wide.region_21.22_spmd, body=%wide.region_18.21_spmd.sunk | while | flops 6052234 | bytes 133554 | solution.py:132
  370.5 26.5 %while.123 = (s32[]{:T(128)}, f32[2,64]{1,0:T(2,128)S(1)}, f32[2,64]{1,0:T(2,128)S(1)}, f32[2,64]{1,0:T(2,128)S(1)}, s32[]{:T(128)}, /*index=5*/f32[2,32768]{1,0...) while((s32[]{:T(128)}, f32[2,64]{1,0:T(2,128)S(1)}, ...), condition=%wide.region_20.20_spmd.clone, body=%wide.region_19.19_spmd.clone.sunk | while | flops 6052232 | bytes 129229 | solution.py:128
  397.1 26.5 %while.123 = (s32[]{:T(128)}, f32[2,64]{1,0:T(2,128)S(1)}, f32[2,64]{1,0:T(2,128)S(1)}, f32[2,64]{1,0:T(2,128)S(1)}, s32[]{:T(128)}, /*index=5*/f32[2,32768]{1,0...) while((s32[]{:T(128)}, f32[2,64]{1,0:T(2,128)S(1)}, ...), condition=%wide.region_20.20_spmd.clone, body=%wide.region_19.19_spmd.clone.sunk | while | flops 6052232 | bytes 129229 | solution.py:128
  423.7 26.5 %while.123 = (s32[]{:T(128)}, f32[2,64]{1,0:T(2,128)S(1)}, f32[2,64]{1,0:T(2,128)S(1)}, f32[2,64]{1,0:T(2,128)S(1)}, s32[]{:T(128)}, /*index=5*/f32[2,32768]{1,0...) while((s32[]{:T(128)}, f32[2,64]{1,0:T(2,128)S(1)}, ...), condition=%wide.region_20.20_spmd.clone, body=%wide.region_19.19_spmd.clone.sunk | while | flops 6052232 | bytes 129229 | solution.py:128
  450.3 26.5 %while.123 = (s32[]{:T(128)}, f32[2,64]{1,0:T(2,128)S(1)}, f32[2,64]{1,0:T(2,128)S(1)}, f32[2,64]{1,0:T(2,128)S(1)}, s32[]{:T(128)}, /*index=5*/f32[2,32768]{1,0...) while((s32[]{:T(128)}, f32[2,64]{1,0:T(2,128)S(1)}, ...), condition=%wide.region_20.20_spmd.clone, body=%wide.region_19.19_spmd.clone.sunk | while | flops 6052232 | bytes 129229 | solution.py:128
  477.6 7.7 %all-to-all-start.6 = ((f32[16,2,256]{2,1,0:T(2,128)}), f32[16,2,256]{2,1,0:T(2,128)S(1)}, u32[]{:S(2)}, u32[]{:S(2)}) async-start(f32[16,2,256]{2,1,0:T(2,128)} %broadcast_in_dim.94), calls=%async_computation.6 | async-start | bytes 65536 | tf_op jit(solution)/shard_map/all_to_all | solution.py:23
  486.1 6.5 %all-to-all-done.6 = f32[16,2,256]{2,1,0:T(2,128)S(1)} async-done(((f32[16,2,256]{2,1,0:T(2,128)}), f32[16,2,256]{2,1,0:T(2,128)S(1)}, u32[]{:S(2)}, u32[]{:S(2)}) %all-to-all-start.6) | async-done | bytes 32800 | tf_op jit(solution)/shard_map/all_to_all | solution.py:23
  493.6 4.8 all-to-all-start.7
  504.5 5.7 %multiply_reduce_fusion.8 = (f32[]{:T(128)}, f32[]{:T(128)}, f32[]{:T(128)}, f32[]{:T(128)}, f32[]{:T(128)}, /*index=5*/f32[]{:T(128)}, f32[]{:T(128)}, f32[]{:T(128)}) fusion(f32[2,256]{1,0:T(2,128)S(1)} %copy-done.5, f32[2,256]{1,0:T(2,128)S(1)} %get-tuple-element.1246, f32[]{:T(128)} %bitcast.64, f32[]{:T(128)} %bitcast.56, f32[]{:T(128)} %bitcast.52, ...), kind=kLoop, calls=%fused_computation.435 | loop fusion | flops 20984 | bytes 8256 | tf_op jit(solution)/shard_map/reduce_sum | solution.py:288
  515.4 3.8 psum.35
  519.1 8.6 %psum.36 = f32[8]{0:T(128)S(1)} all-reduce(f32[8]{0:T(128)S(1)} %psum.35), channel_id=1, replica_groups=mesh['gx_0'=2,'gx_1'=4,'gy_0'=2,'gy_1'=4,'gy_2'=2] {'gx_1'}, use_global_device_ids=true, to_apply=%region_41.42 | all-reduce | flops 8 | bytes 64 | tf_op jit(solution)/shard_map/psum | solution.py:74
  527.8 5.3 psum.37
  533.0 6.9 %psum.38 = f32[8]{0:T(128)S(1)} all-reduce(f32[8]{0:T(128)S(1)} %psum.37), channel_id=1, replica_groups=mesh['gx_0'=2,'gx_1'=4,'gy_0'=2,'gy_1'=4,'gy_2'=2] {'gy_1'}, use_global_device_ids=true, to_apply=%region_43.44 | all-reduce | flops 8 | bytes 64 | tf_op jit(solution)/shard_map/psum | solution.py:74
  540.0 9.4 %psum.39 = f32[8]{0:T(128)S(1)} all-reduce(f32[8]{0:T(128)S(1)} %psum.38), channel_id=1, replica_groups=mesh['gx_0'=2,'gx_1'=4,'gy_0'=2,'gy_1'=4,'gy_2'=2] {'gy_2'}, use_global_device_ids=true, to_apply=%region_44.45 | all-reduce | flops 8 | bytes 64 | tf_op jit(solution)/shard_map/psum | solution.py:74
  (1746 shorter events, 336.4 us)
Async XLA Ops:
  0.6 6.1 %copy-start = (f32[8,4,128]{2,1,0:T(4,128)S(1)}, f32[8,4,128]{2,1,0:T(4,128)}, u32[]{:S(2)}) copy-start(f32[8,4,128]{2,1,0:T(4,128)} %param.20) | copy-start | bytes 49156
  0.6 6.1 %copy-start.1 = (f32[8,4,128]{2,1,0:T(4,128)S(1)}, f32[8,4,128]{2,1,0:T(4,128)}, u32[]{:S(2)}) copy-start(f32[8,4,128]{2,1,0:T(4,128)} %param.19) | copy-start | bytes 49156
  1.4 12.7 %collective-permute-start = (f32[2,1,4,128]{3,2,1,0:T(4,128)S(1)}, f32[2,1,4,128]{3,2,1,0:T(4,128)S(1)}, u32[]{:S(2)}, u32[]{:S(2)}) collective-permute-start(f32[2,1,4,128]{3,2,1,0:T(4,128)S(1)} %get-tuple-element.1341), channel_id=1, source_target_pairs={{0,16},{16,32},{32,48},{48,64},{64,80},{80,96},{96,112},{1,17},{17... | collective-permute-start | bytes 12296 | tf_op jit(solution)/shard_map/ppermute | solution.py:35
  5.4 8.7 %collective-permute-start.1 = (f32[2,1,4,128]{3,2,1,0:T(4,128)S(1)}, f32[2,1,4,128]{3,2,1,0:T(4,128)S(1)}, u32[]{:S(2)}, u32[]{:S(2)}) collective-permute-start(f32[2,1,4,128]{3,2,1,0:T(4,128)S(1)} %get-tuple-element.1342), channel_id=1, source_target_pairs={{16,0},{32,16},{48,32},{64,48},{80,64},{96,80},{112,96},{17,1},{33... | collective-permute-start | bytes 12296 | tf_op jit(solution)/shard_map/ppermute | solution.py:38
  7.5 16.9 %all-to-all-start = ((f32[8,2,8,4,128]{4,3,2,1,0:T(4,128)}), f32[8,2,8,4,128]{4,3,2,1,0:T(4,128)S(1)}, u32[]{:S(2)}, u32[]{:S(2)}) async-start(f32[8,2,8,4,128]{4,3,2,1,0:T(4,128)} %broadcast_in_dim.85), calls=%async_computation | async-start | bytes 524288 | tf_op jit(solution)/shard_map/all_to_all | solution.py:23
  13.4 0.7 copy-start.6
  14.2 6.9 %copy-start.8 = (s32[2,256]{1,0:T(2,128)S(1)}, s32[2,256]{1,0:T(2,128)}, u32[]{:S(2)}) copy-start(s32[2,256]{1,0:T(2,128)} %param.22) | copy-start | bytes 6148
  14.2 7.1 %collective-permute-start.2 = (f32[2,10,1,128]{3,2,1,0:T(1,128)S(1)}, f32[2,10,1,128]{3,2,1,0:T(1,128)S(1)}, u32[]{:S(2)}, u32[]{:S(2)}) collective-permute-start(f32[2,10,1,128]{3,2,1,0:T(1,128)S(1)} %get-tuple-element.1337), channel_id=1, source_target_pairs={{0,1},{1,2},{2,3},{3,4},{4,5},{5,6},{6,7},{7,8},{8,9},{9,10},{10,1... | collective-permute-start | bytes 30728 | tf_op jit(solution)/shard_map/ppermute | solution.py:35
  19.2 5.0 collective-permute-start.3
  131.8 15.8 %all-to-all-start.1 = ((f32[16,2,256]{2,1,0:T(2,128)}), f32[16,2,256]{2,1,0:T(2,128)S(1)}, u32[]{:S(2)}, u32[]{:S(2)}) async-start(f32[16,2,256]{2,1,0:T(2,128)} %broadcast_in_dim.86), calls=%async_computation.1 | async-start | bytes 65536 | tf_op jit(solution)/shard_map/all_to_all | solution.py:23
  140.3 7.3 %copy-start.7 = (f32[2,256]{1,0:T(2,128)S(1)}, f32[2,256]{1,0:T(2,128)}, u32[]{:S(2)}) copy-start(f32[2,256]{1,0:T(2,128)} %param.23) | copy-start | bytes 6148
  148.8 9.9 %all-to-all-start.2 = ((f32[8,4,256]{2,1,0:T(4,128)}), f32[8,4,256]{2,1,0:T(4,128)S(1)}, u32[]{:S(2)}, u32[]{:S(2)}) async-start(f32[8,4,256]{2,1,0:T(4,128)} %broadcast_in_dim.87), calls=%async_computation.2 | async-start | bytes 65536 | tf_op jit(solution)/shard_map/all_to_all | solution.py:23
  158.8 0.7 copy-start.5
  161.0 8.3 %all-to-all-start.3 = ((f32[8,2,256]{2,1,0:T(2,128)}), f32[8,2,256]{2,1,0:T(2,128)S(1)}, u32[]{:S(2)}, u32[]{:S(2)}) async-start(f32[8,2,256]{2,1,0:T(2,128)} %broadcast_in_dim.88), calls=%async_computation.3 | async-start | bytes 32768 | tf_op jit(solution)/shard_map/all_to_all | solution.py:23
  292.5 9.4 %all-to-all-start.4 = ((f32[8,8,2,4,128]{4,3,1,2,0:T(4,128)}), f32[8,8,2,4,128]{4,3,1,2,0:T(4,128)S(1)}, u32[]{:S(2)}, u32[]{:S(2)}) async-start(f32[8,8,2,4,128]{4,3,1,2,0:T(4,128)} %copy.54), calls=%async_computation.4 | async-start | bytes 524288 | tf_op jit(solution)/shard_map/all_to_all | solution.py:62
  302.0 39.5 %copy-start.2 = (f32[8,2,4,128]{3,2,0,1:T(4,128)}, f32[8,2,4,128]{3,2,0,1:T(4,128)S(1)}, u32[]{:S(2)}) copy-start(f32[8,2,4,128]{3,2,0,1:T(4,128)S(1)} %reduce_sum.201) | copy-start | bytes 98308
  302.6 38.9 %copy-start.3 = (f32[2,8,4,128]{3,2,1,0:T(4,128)}, f32[2,8,4,128]{3,2,1,0:T(4,128)S(1)}, u32[]{:S(2)}) copy-start(f32[2,8,4,128]{3,2,1,0:T(4,128)S(1)} %get-tuple-element.1224) | copy-start | bytes 98308
  341.5 4.2 collective-permute-start.4
  344.3 4.4 collective-permute-start.5
  348.7 6.0 %copy-start.4 = (f32[8]{0:T(128)S(1)}, f32[8]{0:T(128)}, u32[]{:S(2)}) copy-start(f32[8]{0:T(128)} %param.25) | copy-start | bytes 100
  348.7 13.3 %collective-permute-start.6 = (f32[2,10,1,128]{3,2,1,0:T(1,128)S(1)}, f32[2,10,1,128]{3,2,1,0:T(1,128)S(1)}, u32[]{:S(2)}, u32[]{:S(2)}) collective-permute-start(f32[2,10,1,128]{3,2,1,0:T(1,128)S(1)} %get-tuple-element.1335), channel_id=1, source_target_pairs={{0,1},{1,2},{2,3},{3,4},{4,5},{5,6},{6,7},{7,8},{8,9},{9,10},{10,1... | collective-permute-start | bytes 30728 | tf_op jit(solution)/shard_map/ppermute | solution.py:35
  352.8 9.3 %collective-permute-start.7 = (f32[2,10,1,128]{3,2,1,0:T(1,128)S(1)}, f32[2,10,1,128]{3,2,1,0:T(1,128)S(1)}, u32[]{:S(2)}, u32[]{:S(2)}) collective-permute-start(f32[2,10,1,128]{3,2,1,0:T(1,128)S(1)} %get-tuple-element.1336), channel_id=1, source_target_pairs={{1,0},{2,1},{3,2},{4,3},{5,4},{6,5},{7,6},{8,7},{9,8},{10,9},{11,1... | collective-permute-start | bytes 30728 | tf_op jit(solution)/shard_map/ppermute | solution.py:38
  356.2 14.0 %all-to-all-start.5 = ((f32[8,2,8,4,128]{4,3,2,1,0:T(4,128)}), f32[8,2,8,4,128]{4,3,2,1,0:T(4,128)S(1)}, u32[]{:S(2)}, u32[]{:S(2)}) async-start(f32[8,2,8,4,128]{4,3,2,1,0:T(4,128)} %broadcast_in_dim.93), calls=%async_computation.5 | async-start | bytes 524288 | tf_op jit(solution)/shard_map/all_to_all | solution.py:23
  477.6 15.0 %all-to-all-start.6 = ((f32[16,2,256]{2,1,0:T(2,128)}), f32[16,2,256]{2,1,0:T(2,128)S(1)}, u32[]{:S(2)}, u32[]{:S(2)}) async-start(f32[16,2,256]{2,1,0:T(2,128)} %broadcast_in_dim.94), calls=%async_computation.6 | async-start | bytes 65536 | tf_op jit(solution)/shard_map/all_to_all | solution.py:23
  493.6 10.5 %all-to-all-start.7 = ((f32[8,2,256]{2,1,0:T(2,128)}), f32[8,2,256]{2,1,0:T(2,128)S(1)}, u32[]{:S(2)}, u32[]{:S(2)}) async-start(f32[8,2,256]{2,1,0:T(2,128)} %broadcast_in_dim.95), calls=%async_computation.7 | async-start | bytes 32768 | tf_op jit(solution)/shard_map/all_to_all | solution.py:23
where the time goes:
time: 552 us; the launch traced here: 550 us
  matrix products  278 us (50%)
  blocking collectives  72.1 us (13%)
  starting transfers between devices  66.6 us (12%)
  other arithmetic  37.7 us (7%)
  waiting for transfers between devices  35.5 us (6%)
  local copies, waits for them, and re-layouts  29.1 us (5%)
  loops' own time  19.2 us (3%)
  between operations  12 us (2%)
    dot_general x256, matrix products, forward_cell_turn(): jnp.dot(kernel_tile(field, block_x[field], block_y[field], cell_x, cell_y...  195 us
    dot_general x128, matrix products, cell_station_turn(): jnp.dot(block_source[field], kernel_tile(field, block_x[field], block_y[f...  80.4 us
    all_to_all x7, starting transfers between devices, from_everyone(): return lax.all_to_all(copies, axis, split_axis=0, concat_axis=0, tiled=True)  40.9 us
    pmax x5, blocking collectives, over_axes(): value = lax.pmax(value, axis)  38.2 us
    psum x5, blocking collectives, over_axes_2(): value = lax.psum(value, axis)  34 us
    all_to_all x7, waiting for transfers between devices, from_everyone(): return lax.all_to_all(copies, axis, split_axis=0, concat_axis=0, tiled=True)  23.8 us
    ppermute x4, starting transfers between devices, extended_2(): lax.ppermute(lax.slice_in_dim(block, block.shape[dim] - width, None, axis...  15.9 us
  transfers between devices with their start and end apart: 16, of which 7 were waited for; matrix products, arithmetic and copies ran while one was open for 2% of the time, Pallas kernels for 0%

commit v1 on v0

v1 whole, which is shorter than its diff:
```python
import jax
import jax.numpy as jnp
from jax import lax
from jax.experimental import pallas as pl
from jax.experimental.pallas import tpu as pltpu
from jax.sharding import Mesh
from jax.sharding import PartitionSpec as P

AXES = ("xl", "y", "xh", "z", "c")
GX = ("xl", "y")
GY = ("xh", "z", "c")

NX = 64
NY = 64
NZ = 128
STATIONS = 2048
LINES = 256
TRIALS = 8
SIDE = 8
PAD = 8
US = NX + PAD
LANES = 128
cell_depth = 2.0
lift = 1.0
coupling = 0.05 * STATIONS / (NX * NY * NZ)

f32 = jnp.float32
bf16 = jnp.bfloat16
MESH = pl.DeviceIdType.MESH


def split(value):
    high = value.astype(bf16)
    low = (value - high.astype(f32)).astype(bf16)
    return high, low


def rounded(value):
    high = value.astype(bf16).astype(f32)
    return high, value - high


def dot(a, b):
    return jnp.dot(a, b, preferred_element_type=f32)


def dot_nt(a, b):
    return lax.dot_general(a, b, (((1,), (1,)), ((), ())), preferred_element_type=f32)


def iota(shape, axis):
    return lax.broadcasted_iota(jnp.int32, shape, axis)


def kernel(
    den, sus, cell, line, obs, wgt, steps,
    dg_out, cf_out, wr_out, tv_out,
    blk, cell_v, line_v, obs_v, wgt_v, st, rowv, tt, ar1, ar2, ar3,
    ohx, ohy, ohl, xlo, xhi, ylo_s, yhi_s, ylo, yhi, big,
    e_hi, e_lo, x_hi, x_lo, sgp, dgb, cfb, cfo, dgo, wr_all, wrx, wro, fin, tvo, inv_cnt,
    load_sem, out_sem, pair_send, pair_recv, st_send, st_recv,
    a1_send, a1_recv, a2_send, a2_recv, a3_send, a3_recv, halo_send, halo_recv,
):
    xl, y, xh, z, c = (lax.axis_index(a) for a in AXES)
    bx = xl * 4 + y
    by = xh * 4 + z
    px = xh * 2 + xl
    i0 = bx * SIDE
    j0 = by * SIDE
    pending = []

    def remote(src, dst, send, recv, device):
        return pltpu.make_async_remote_copy(
            src_ref=src, dst_ref=dst, send_sem=send, recv_sem=recv, device_id=device, device_id_type=MESH
        )

    def start(copy):
        copy.start()
        pending.append(copy)

    loads = [
        pltpu.make_async_copy(den, blk.at[c, 0], load_sem.at[0]),
        pltpu.make_async_copy(sus, blk.at[c, 1], load_sem.at[1]),
        pltpu.make_async_copy(cell, cell_v, load_sem.at[2]),
        pltpu.make_async_copy(line, line_v, load_sem.at[3]),
        pltpu.make_async_copy(obs, obs_v, load_sem.at[4]),
        pltpu.make_async_copy(wgt, wgt_v, load_sem.at[5]),
    ]
    for copy in loads:
        copy.start()
    barrier = pltpu.get_barrier_semaphore()
    partner = {"c": 1 - c}
    pl.semaphore_signal(barrier, inc=1, device_id=partner, device_id_type=MESH)
    for d in range(1, 8):
        q = (bx + d) % 8
        pl.semaphore_signal(barrier, inc=1, device_id={"xl": q // 4, "y": q % 4}, device_id_type=MESH)
        q = (by + d) % 8
        pl.semaphore_signal(barrier, inc=1, device_id={"xh": q // 4, "z": q % 4}, device_id_type=MESH)
    pl.semaphore_signal(barrier, inc=1, device_id={"xl": 1 - xl, "xh": 1 - xh}, device_id_type=MESH)

    for copy in loads:
        copy.wait()
    rows = []
    for ref in (cell_v, line_v, obs_v, wgt_v):
        value = ref[...].astype(f32)
        row = jnp.where(c == 0, value[0:1], value[1:2])
        rows += [row[:, :LANES], row[:, LANES:]]
    st[bx] = jnp.concatenate(rows, axis=0)
    big[...] = jnp.zeros_like(big)

    lane = iota((1, LANES), 1)
    dy = (NY - 1 - lane - j0).astype(f32)
    dx = (iota((US, 1), 0) - PAD - i0).astype(f32)
    rowv[...] = dx * dx + dy * dy

    def table_rows(tile, carry):
        depth = ((tile * 16 + iota((16, LANES), 0)).astype(f32) + 0.5) * cell_depth + lift
        square = depth * depth
        scale = jnp.where(c == 0, 0.0, 3.0 * square)
        shift = jnp.where(c == 0, depth, -1.0)
        first = pl.multiple_of(tile * 16, 16)
        for u in range(US):
            inverse = lax.rsqrt(square + rowv[u : u + 1, :])
            inv2 = inverse * inverse
            value = inv2 * inverse * (scale * inv2 + shift)
            high, low = split(value)
            tt[pl.ds(first, 16), u * LANES : (u + 1) * LANES] = high
            tt[pl.ds(first + NZ, 16), u * LANES : (u + 1) * LANES] = low
        return carry

    lax.fori_loop(0, 4, table_rows, 0)

    pl.semaphore_wait(barrier, 16)
    pair_blk = remote(blk.at[c], blk.at[c], pair_send.at[0], pair_recv.at[0], partner)
    start(pair_blk)
    for d in range(1, 8):
        q = (bx + d) % 8
        start(remote(st.at[bx], st.at[bx], st_send.at[d - 1], st_recv.at[bx], {"xl": q // 4, "y": q % 4}))

    lax.fori_loop(4, 8, table_rows, 0)

    pair_blk.wait_recv()
    qm = (bx + 7) % 8
    qp = (bx + 1) % 8
    left = {"xl": qm // 4, "y": qm % 4}
    right = {"xl": qp // 4, "y": qp % 4}
    halo_l = remote(blk.at[:, :, 0:2], xhi, halo_send.at[0], halo_recv.at[0], left)
    halo_r = remote(blk.at[:, :, 7:8], xlo, halo_send.at[1], halo_recv.at[1], right)
    start(halo_l)
    start(halo_r)

    def forward(columns):
        cells = jnp.concatenate([v.reshape(SIDE, 1, NZ) for v in columns], axis=1).reshape(SIDE * SIDE, NZ)
        high, low = split(cells)
        lhs = jnp.concatenate(
            [jnp.concatenate([high, high], axis=1), jnp.concatenate([low, jnp.zeros_like(low)], axis=1)], axis=0
        )
        sums = [None] * NX
        for t in range(US // 8):
            part = dot(lhs, tt[:, t * 8 * LANES : (t + 1) * 8 * LANES])
            part = part[: SIDE * SIDE] + part[SIDE * SIDE :]
            for uu in range(8):
                for i in range(SIDE):
                    x = t * 8 + uu - PAD + i
                    if 0 <= x < NX:
                        piece = part[i * SIDE : (i + 1) * SIDE, uu * LANES : (uu + 1) * LANES]
                        sums[x] = piece if sums[x] is None else sums[x] + piece
        grid = []
        for x in range(NX):
            turned = pltpu.roll(sums[x], 121, 1, stride=1, stride_axis=0)
            grid.append(jnp.sum(turned, axis=0, keepdims=True))
        upper = jnp.concatenate(grid[: NX // 2], axis=0)
        lower = jnp.concatenate(grid[NX // 2 :], axis=0)
        return jnp.where(lane < NY, upper, pltpu.roll(lower, NY, 1))

    def line_copies(buf, sends, recvs, stage):
        me = (px, y, z)[stage]
        copies = []
        for d in range(1, 4):
            q = (me + d) % 4
            device = ({"xh": q // 2, "xl": q % 2}, {"y": q}, {"z": q})[stage]
            out = remote(buf.at[stage, me], buf.at[stage, me], sends.at[stage, d - 1], recvs.at[stage, me], device)
            into = remote(buf.at[stage, q], buf.at[stage, q], sends.at[stage, d - 1], recvs.at[stage, q], device)
            copies.append((out, into))
        return me, copies

    def line_start(buf, sends, recvs, stage, value):
        me, copies = line_copies(buf, sends, recvs, stage)
        buf[stage, me] = value
        for out, _ in copies:
            start(out)
        return copies

    def line_wait(copies):
        for _, into in copies:
            into.wait_recv()

    def line_sum(buf, stage):
        return (buf[stage, 0] + buf[stage, 1]) + (buf[stage, 2] + buf[stage, 3])

    halves = [blk[core, c] for core in range(2)]
    columns = [halves[q // 4][:, q % 4, :] for q in reversed(range(SIDE))]
    first = line_start(ar1, a1_send, a1_recv, 0, forward(columns))

    for d in range(1, 8):
        q = (bx + d) % 8
        remote(st.at[q], st.at[q], st_send.at[d - 1], st_recv.at[q], partner).wait_recv()

    def station_row(index):
        return jnp.concatenate(
            [st[g, 2 * index + h : 2 * index + h + 1, :] for g in range(8) for h in range(2)], axis=1
        )

    station = station_row(0).astype(jnp.int32)
    station_x = station // NY
    station_m = NY - 1 - station % NY
    labels = station_row(1).astype(jnp.int32)
    label_h = labels // LANES
    label_l = labels % LANES
    data = station_row(2)
    weight = station_row(3)
    one = lambda mask: jnp.where(mask, 1.0, 0.0).astype(bf16)
    ohy[...] = one(iota((LANES, STATIONS), 0) == station_m)
    ohl[...] = one(iota((LANES, STATIONS), 0) == label_l)
    hmask = iota((8, STATIONS), 0) == label_h
    xmask = iota((NX, STATIONS), 0) == station_x
    hot = jnp.where(hmask, 1.0, 0.0)
    counts = dot_nt(jnp.concatenate([hot, jnp.zeros_like(hot)], axis=0).astype(bf16), ohl[...])[:8]
    inv_cnt[...] = 1.0 / jnp.maximum(counts, 1.0)

    line_wait(first)
    second = line_start(ar1, a1_send, a1_recv, 1, line_sum(ar1, 0))

    halo_l.wait_recv()
    halo_r.wait_recv()
    for f in range(2):
        for core in range(2):
            at = slice(1 + 4 * core, 5 + 4 * core)
            big[f, 1:9, at, :] = blk[core, f]
            big[f, 0:1, at, :] = xlo[core, f]
            big[f, 9:11, at, :] = xhi[core, f]
    ylo_s[...] = big[:, :, 1:3, :]
    yhi_s[...] = big[:, :, 8:9, :]
    qm = (by + 7) % 8
    qp = (by + 1) % 8
    halo_d = remote(ylo_s, yhi, halo_send.at[2], halo_recv.at[2], {"xh": qm // 4, "z": qm % 4})
    halo_u = remote(yhi_s, ylo, halo_send.at[3], halo_recv.at[3], {"xh": qp // 4, "z": qp % 4})
    start(halo_d)
    start(halo_u)

    line_wait(second)
    third = line_start(ar1, a1_send, a1_recv, 2, line_sum(ar1, 1))

    halo_d.wait_recv()
    halo_u.wait_recv()
    big[:, :, 9:11, :] = yhi[...]
    big[:, :, 0:1, :] = ylo[...]

    ni, nj = SIDE + 2, 16
    deep = iota((1, 1, NZ), 2) < NZ - 1
    gi = i0 - 1 + iota((ni, nj, NZ), 0)
    gj = j0 - 1 + iota((ni, nj, NZ), 1)
    along_i = gi < NX - 1
    along_j = gj < NY - 1
    valid = (gi >= 0) & (gj >= 0)

    def roll_j(value, shift):
        n = value.shape[0]
        return pltpu.roll(value, shift, 1)

    def roll_k(value, shift):
        return pltpu.roll(value, shift, 2)

    def diffs(value, mask_i, mask_j):
        base = value[:-1]
        return (
            jnp.where(mask_i, value[1:] - base, 0.0),
            jnp.where(mask_j, roll_j(base, nj - 1) - base, 0.0),
            jnp.where(deep, roll_k(base, NZ - 1) - base, 0.0),
        )

    def cross(a, b):
        return (a[1] * b[2] - a[2] * b[1], a[2] * b[0] - a[0] * b[2], a[0] * b[1] - a[1] * b[0])

    def inner(a, b):
        return a[0] * b[0] + a[1] * b[1] + a[2] * b[2]

    a = diffs(big[0], along_i, along_j)
    b = diffs(big[1], along_i, along_j)
    t = tuple(jnp.where(valid, v, 0.0) for v in cross(a, b))
    for f, pull in enumerate((cross(b, t), cross(t, a))):
        px_ = jnp.where(along_i, pull[0], 0.0)
        py_ = jnp.where(along_j, pull[1], 0.0)
        pz_ = jnp.where(deep, pull[2], 0.0)
        force = px_[:-1] - px_[1:]
        force = force + (roll_j(py_, 1) - py_)[1:]
        force = force + (jnp.where(iota((1, 1, NZ), 2) > 0, roll_k(pz_, 1), 0.0) - pz_)[1:]
        force = roll_j(force, nj - 1)
        cfb[f] = force
        cfo[f] = jnp.where(c == 0, force[:SIDE, 0:4], force[:SIDE, 4:8])
    out_cf = pltpu.make_async_copy(cfo, cf_out, out_sem.at[0])
    out_cf.start()

    line_wait(third)
    predicted = line_sum(ar1, 2)

    def gather(packed):
        both = jnp.concatenate([packed, pltpu.roll(packed, NY, 1)], axis=0)
        high, low = split(both)
        hit = dot(jnp.concatenate([high, low], axis=0), ohy[...])
        hit = hit[:NX] + hit[NX:]
        return jnp.sum(jnp.where(xmask, hit, 0.0), axis=0, keepdims=True)

    def masked_split(mask, value):
        high, low = rounded(value)
        return jnp.concatenate([jnp.where(mask, high, 0.0), jnp.where(mask, low, 0.0)], axis=0).astype(bf16)

    def level(value):
        sums = dot_nt(masked_split(hmask, value), ohl[...])
        means = (sums[:8] + sums[8:]) * inv_cnt[...]
        high, low = split(means)
        spread = dot(jnp.concatenate([high, low], axis=0), ohl[...])
        spread = spread[:8] + spread[8:]
        return value - jnp.sum(jnp.where(hmask, spread, 0.0), axis=0, keepdims=True)

    residual = level(gather(predicted) - data)
    weighted = weight * residual
    source = level(weight * weighted)

    hits = dot_nt(masked_split(xmask, source), ohy[...])
    sg = hits[:NX] + hits[NX:]
    zero = jnp.zeros((PAD, LANES), f32)
    parts = rounded(sg)
    for part, shifts, extra in zip(parts, (e_hi, e_lo), (x_hi, x_lo)):
        turned = [zero] * PAD
        for x in range(NX):
            row = jnp.broadcast_to(part[x : x + 1], (SIDE, LANES))
            turned.append(pltpu.roll(row, 0, 1, stride=1, stride_axis=0))
        turned += [zero] * (PAD + 2)
        for n in range(US + 8):
            shifts[:, n * LANES : (n + 1) * LANES] = jnp.concatenate([turned[n], turned[n + 1]], axis=0).astype(bf16)
        sgp[0:PAD] = zero
        sgp[PAD : PAD + NX] = pltpu.roll(part, SIDE, 1)
        sgp[PAD + NX : PAD + NX + 16] = jnp.zeros((16, LANES), f32)
        for u in range(US):
            extra[:, u * LANES : (u + 1) * LANES] = sgp[u : u + 16].astype(bf16)

    acc = None
    for t in range(US // 2):
        lanes = [slice((2 * t + 2 * p) * LANES, (2 * t + 2 * p + 2) * LANES) for p in range(5)]
        lhs = jnp.concatenate(
            [e_hi[:, s] for s in lanes] + [x_hi[:, lanes[0]]] + [e_lo[:, s] for s in lanes] + [x_lo[:, lanes[0]]],
            axis=0,
        )
        term = dot_nt(lhs, tt[:, lanes[0]])
        acc = term if acc is None else acc + term
    dg = acc[:96, :NZ] + acc[:96, NZ:] + acc[96:, :NZ]
    main = dg[:80].reshape(10, SIDE, NZ)
    dgb[c, :, 0:SIDE, :] = main
    for i in range(SIDE + 1):
        dgb[c, i, SIDE : SIDE + 1, :] = dg[80 + i : 81 + i]
    pair_dg = remote(dgb.at[c], dgb.at[c], pair_send.at[1], pair_recv.at[1], partner)
    start(pair_dg)

    own = main[:SIDE] + coupling * cfb[c, 0:SIDE, 0:SIDE, :]
    columns = [own[:, q, :] for q in reversed(range(SIDE))]
    first = line_start(ar2, a2_send, a2_recv, 0, forward(columns))

    for g in range(8):
        for h in range(2):
            at = (2 * g + h) * LANES
            wr_all[g, h : h + 1, :] = weighted[:, at : at + LANES]
    wrx[c] = wr_all[bx]
    pair_wr = remote(wrx.at[c], wrx.at[c], pair_send.at[2], pair_recv.at[2], partner)
    start(pair_wr)

    pair_dg.wait_recv()
    for f in range(2):
        dgo[f] = jnp.where(c == 0, dgb[f, 0:SIDE, 0:4, :], dgb[f, 0:SIDE, 4:8, :])
    out_dg = pltpu.make_async_copy(dgo, dg_out, out_sem.at[1])
    out_dg.start()

    grads = [dgb[f, 0 : SIDE + 1] + coupling * cfb[f] for f in range(2)]
    edge_i = i0 + iota((SIDE, nj, NZ), 0) < NX - 1
    edge_j = j0 + iota((SIDE, nj, NZ), 1) < NY - 1
    models = [roll_j(big[f, 1:10], nj - 1) for f in range(2)]

    def short(value):
        return tuple(v[:, 0:SIDE] for v in diffs(value, edge_i, edge_j))

    am, bm, ag, bg = (short(v) for v in (*models, *grads))
    t0 = cross(am, bm)
    t1 = tuple(p + q for p, q in zip(cross(ag, bm), cross(am, bg)))
    t2 = cross(ag, bg)
    energy = (
        inner(t0, t0),
        -2.0 * inner(t0, t1),
        inner(t1, t1) + 2.0 * inner(t0, t2),
        -2.0 * inner(t1, t2),
        inner(t2, t2),
    )
    terms = [jnp.sum(jnp.sum(e, axis=0), axis=0, keepdims=True) for e in energy]
    largest = jnp.maximum(jnp.abs(grads[0][:SIDE, 0:SIDE]), jnp.abs(grads[1][:SIDE, 0:SIDE]))
    terms.append(jnp.max(jnp.max(largest, axis=0), axis=0, keepdims=True))
    terms.append(jnp.zeros((2, LANES), f32))
    small = jnp.concatenate(terms, axis=0)
    is_peak = iota((8, LANES), 0) == 5

    def small_sum(stage):
        p, q, r, s = (ar3[stage, n] for n in range(4))
        top = jnp.maximum(jnp.maximum(p, q), jnp.maximum(r, s))
        return jnp.where(is_peak, top, (p + q) + (r + s))

    line_wait(first)
    second = line_start(ar2, a2_send, a2_recv, 1, line_sum(ar2, 0))
    small_1 = line_start(ar3, a3_send, a3_recv, 0, small)
    pair_wr.wait_recv()
    for f in range(2):
        for h in range(2):
            wro[f : f + 1, h * LANES : (h + 1) * LANES] = wrx[f, h : h + 1, :]
    out_wr = pltpu.make_async_copy(wro, wr_out, out_sem.at[2])
    out_wr.start()
    line_wait(second)
    third = line_start(ar2, a2_send, a2_recv, 2, line_sum(ar2, 1))
    line_wait(small_1)
    small_2 = line_start(ar3, a3_send, a3_recv, 1, small_sum(0))
    line_wait(third)
    image = line_sum(ar2, 2)
    line_wait(small_2)
    small_3 = line_start(ar3, a3_send, a3_recv, 2, small_sum(1))
    change = level(gather(image))
    line_wait(small_3)
    small = small_sum(2)

    peak = jnp.max(small, axis=1, keepdims=True)[5:6] + 1e-06
    totals = jnp.sum(small, axis=1, keepdims=True)
    tau = jnp.zeros((TRIALS, LANES), f32)
    for k in range(TRIALS):
        tau = jnp.where(iota((TRIALS, LANES), 0) == k, steps[k], tau)
    tau = tau / peak
    moved = weight * (residual - tau[:, 0:1] * change)
    value = 0.5 * jnp.sum(moved * moved, axis=1, keepdims=True)
    fin[c] = jnp.broadcast_to(value, (TRIALS, LANES))
    pair_fin = remote(fin.at[c], fin.at[c], pair_send.at[3], pair_recv.at[3], partner)
    start(pair_fin)
    poly = totals[4:5]
    for n in (3, 2, 1, 0):
        poly = poly * tau + totals[n : n + 1]
    pair_fin.wait_recv()
    tvo[...] = ((fin[0] + fin[1]) + coupling * 0.5 * poly) / (2.0 * STATIONS)
    out_tv = pltpu.make_async_copy(tvo, tv_out, out_sem.at[3])
    out_tv.start()
    for copy in pending:
        copy.wait_send()
    for copy in (out_cf, out_dg, out_wr, out_tv):
        copy.wait()


def body(density, susceptibility, station_cell, station_line, observed, data_weight, trial_steps):
    hbm = pl.BlockSpec(memory_space=pl.ANY)
    vmem = lambda *shape: pltpu.VMEM(shape, f32)
    half = lambda *shape: pltpu.VMEM(shape, bf16)
    sem = lambda *shape: pltpu.SemaphoreType.DMA(shape)
    scratch = [
        vmem(2, 2, SIDE, 4, NZ),
        pltpu.VMEM((2, 256), jnp.int32), pltpu.VMEM((2, 256), jnp.int32), vmem(2, 256), vmem(2, 256),
        vmem(8, 8, LANES),
        vmem(US, LANES),
        half(2 * NZ, US * LANES),
        vmem(3, 4, NX // 2, LANES), vmem(3, 4, NX // 2, LANES), vmem(3, 4, 8, LANES),
        half(NX, STATIONS), half(LANES, STATIONS), half(LANES, STATIONS),
        vmem(2, 2, 1, 4, NZ), vmem(2, 2, 2, 4, NZ),
        vmem(2, 11, 2, NZ), vmem(2, 11, 1, NZ), vmem(2, 11, 1, NZ), vmem(2, 11, 2, NZ),
        vmem(2, 11, 16, NZ),
        half(16, (US + 8) * LANES), half(16, (US + 8) * LANES), half(16, US * LANES), half(16, US * LANES),
        vmem(PAD + NX + 16, LANES),
        vmem(2, 10, 16, NZ), vmem(2, SIDE + 1, 16, NZ),
        vmem(2, SIDE, 4, NZ), vmem(2, SIDE, 4, NZ),
        vmem(8, 2, LANES), vmem(2, 2, LANES), vmem(2, 256), vmem(2, TRIALS, LANES), vmem(TRIALS, LANES),
        vmem(8, LANES),
        sem(6), sem(4), sem(4), sem(4), sem(7), sem(8),
        sem(3, 3), sem(3, 4), sem(3, 3), sem(3, 4), sem(3, 3), sem(3, 4), sem(4), sem(4),
    ]
    shape = lambda *s: jax.ShapeDtypeStruct(s, f32)
    dg, cf, wr, tv = pl.pallas_call(
        kernel,
        out_shape=(shape(2, SIDE, 4, NZ), shape(2, SIDE, 4, NZ), shape(2, 256), shape(TRIALS, LANES)),
        in_specs=[hbm] * 6 + [pl.BlockSpec(memory_space=pltpu.SMEM)],
        out_specs=(hbm,) * 4,
        scratch_shapes=scratch,
        compiler_params=pltpu.CompilerParams(
            collective_id=0, has_side_effects=True, vmem_limit_bytes=48 * 1024 * 1024
        ),
    )(density, susceptibility, station_cell, station_line, observed, data_weight, trial_steps)
    return dg, cf, wr, tv[:, 0]


def solution(mesh):
    torus = Mesh(mesh.devices.reshape(2, 4, 2, 4, 2), AXES)
    in_specs = (
        P(GX, GY, None), P(GX, GY, None), P(None, GX), P(None, GX), P(None, GX), P(None, GX), P(),
    )
    out_specs = (P(None, GX, GY, None), P(None, GX, GY, None), P(None, GX), P())
    return jax.shard_map(body, mesh=torus, in_specs=in_specs, out_specs=out_specs, check_vma=False)
```

time: 552 us -> 52.9 us (0.10)
  matrix products: 278 us -> 0 us
  blocking collectives: 72.1 us -> 0 us
  starting transfers between devices: 66.6 us -> 0 us
  Pallas kernels: 0 us -> 44.7 us
  other arithmetic: 37.7 us -> 0 us
  waiting for transfers between devices: 35.5 us -> 0 us
  local copies, waits for them, and re-layouts: 29.1 us -> 7.24 us
  loops' own time: 19.2 us -> 0 us
  between operations: 12 us -> 0.66 us
    dot_general x390 -> x0, matrix products: 278 us -> none  [the longest x256 195 us: forward_cell_turn(): jnp.dot(kernel_tile(field, block_x[field], block_y[field], cell_x, cell_y...]
    pallas_call x0 -> x1, Pallas kernels: none -> 44.7 us  [body(): pl.pallas_call(kernel, out_shape=(shape(2, SIDE, 4, NZ), shape(2, SIDE, 4...]
    all_to_all x8 -> x0, starting transfers between devices: 44.3 us -> none  [the longest x7 40.9 us: from_everyone(): return lax.all_to_all(copies, axis, split_axis=0, concat_axis=0, tiled=True)]
    pmax x5 -> x0, blocking collectives: 38.2 us -> none  [over_axes(): value = lax.pmax(value, axis)]
    psum x5 -> x0, blocking collectives: 34 us -> none  [over_axes_2(): value = lax.psum(value, axis)]
    all_to_all x8 -> x0, waiting for transfers between devices: 29.7 us -> none  [the longest x7 23.8 us: from_everyone(): return lax.all_to_all(copies, axis, split_axis=0, concat_axis=0, tiled=True)]
    ppermute x8 -> x0, starting transfers between devices: 22.3 us -> none  [the longest x4 15.9 us: extended_2(): lax.ppermute(lax.slice_in_dim(block, block.shape[dim] - width, None, axis...]
    another operation x27 -> x0, loops' own time: 19.2 us -> none  [the longest x1 11 us: adjoint_part(): lax.map(adjoint_cell_turn, jnp.arange(cells // cell_block, dtype=jnp.int32))]
  transfers between devices with their start and end apart: 16 -> 0, of which waited for: 7 -> 0; matrix products, arithmetic and copies ran while one was open for 2% -> 0% of each run, Pallas kernels for 0% -> 0%
where the time goes in v1:
time: 52.9 us; the launch traced here: 52.6 us
  Pallas kernels  44.7 us (84%)
  local copies, waits for them, and re-layouts  7.24 us (14%)
  between operations  0.66 us (1%)
    pallas_call x1, Pallas kernels, body(): pl.pallas_call(kernel, out_shape=(shape(2, SIDE, 4, NZ), shape(2, SIDE, 4...  44.7 us
    unnamed x17, local copies, waits for them, and re-layouts  6.61 us

profile of v1, /device:TPU:1, one launch (start us, length us, event | category | flops | bytes accessed | tf_op | source)
XLA Modules:
  0.0 52.6 jit_solution(11552893684545441517)
XLA Ops:
  0.6 0.0 copy-start
  0.6 0.7 %copy-done = f32[8,4,128]{2,1,0:T(4,128)S(1)} copy-done((f32[8,4,128]{2,1,0:T(4,128)S(1)}, f32[8,4,128]{2,1,0:T(4,128)}, u32[]{:S(2)}) %copy-start) | copy-done | bytes 16408
  1.4 0.0 copy-start.1
  1.4 0.7 %copy-done.1 = f32[8,4,128]{2,1,0:T(4,128)S(1)} copy-done((f32[8,4,128]{2,1,0:T(4,128)S(1)}, f32[8,4,128]{2,1,0:T(4,128)}, u32[]{:S(2)}) %copy-start.1) | copy-done | bytes 16408
  2.1 0.0 copy-start.2
  2.1 0.7 %copy-done.2 = s32[2,256]{1,0:T(2,128)S(1)} copy-done((s32[2,256]{1,0:T(2,128)S(1)}, s32[2,256]{1,0:T(2,128)}, u32[]{:S(2)}) %copy-start.2) | copy-done | bytes 2072
  2.8 0.0 copy-start.3
  2.8 0.7 %copy-done.3 = s32[2,256]{1,0:T(2,128)S(1)} copy-done((s32[2,256]{1,0:T(2,128)S(1)}, s32[2,256]{1,0:T(2,128)}, u32[]{:S(2)}) %copy-start.3) | copy-done | bytes 2072
  3.4 0.0 copy-start.4
  3.4 0.7 %copy-done.4 = f32[2,256]{1,0:T(2,128)S(1)} copy-done((f32[2,256]{1,0:T(2,128)S(1)}, f32[2,256]{1,0:T(2,128)}, u32[]{:S(2)}) %copy-start.4) | copy-done | bytes 2072
  4.1 0.0 copy-start.5
  4.1 0.7 %copy-done.5 = f32[2,256]{1,0:T(2,128)S(1)} copy-done((f32[2,256]{1,0:T(2,128)S(1)}, f32[2,256]{1,0:T(2,128)}, u32[]{:S(2)}) %copy-start.5) | copy-done | bytes 2072
  4.8 0.0 copy-start.6
  4.8 0.7 %copy-done.6 = f32[8]{0:T(128)S(1)} copy-done((f32[8]{0:T(128)S(1)}, f32[8]{0:T(128)}, u32[]{:S(2)}) %copy-start.6) | copy-done | bytes 56
  5.5 44.7 %shard_map.102 = (f32[2,8,4,128]{3,2,1,0:T(4,128)S(1)}, f32[2,8,4,128]{3,2,1,0:T(4,128)S(1)}, f32[2,256]{1,0:T(2,128)S(1)}, f32[8,128]{1,0:T(8,128)S(1)}) custom-call(f32[8,4,128]{2,1,0:T(4,128)S(1)} %copy-done, f32[8,4,128]{2,1,0:T(4,128)S(1)} %copy-done.1, s32[2,256]{1,0:T(2,128)S(1)} %copy-done.2, s32[2,256]{1,0:T(2,128)S(1)} %copy-done.3, ...), custom_call_target="tpu_custom_call" | custom-call | tf_op jit(solution)/shard_map/pallas_call | solution.py:485
  50.1 0.6 %slice_reduce_fusion = f32[8]{0:T(128)} fusion(f32[8,128]{1,0:T(8,128)S(1)} %get-tuple-element.11), kind=kLoop, calls=%fused_computation | loop fusion | bytes 64 | tf_op jit(solution)/shard_map/slice | solution.py:495
  50.8 0.6 %copy.14 = f32[2,8,4,128]{3,2,1,0:T(4,128)} copy(f32[2,8,4,128]{3,2,1,0:T(4,128)S(1)} %get-tuple-element.16) | data formatting | bytes 65536
  51.4 0.6 %copy.15 = f32[2,8,4,128]{3,2,1,0:T(4,128)} copy(f32[2,8,4,128]{3,2,1,0:T(4,128)S(1)} %get-tuple-element.17) | data formatting | bytes 65536
  52.0 0.6 %copy.16 = f32[2,256]{1,0:T(2,128)} copy(f32[2,256]{1,0:T(2,128)S(1)} %get-tuple-element.18) | data formatting | bytes 4096
Async XLA Ops:
  0.6 0.7 %copy-start = (f32[8,4,128]{2,1,0:T(4,128)S(1)}, f32[8,4,128]{2,1,0:T(4,128)}, u32[]{:S(2)}) copy-start(f32[8,4,128]{2,1,0:T(4,128)} %den.1) | copy-start | bytes 49156
  1.4 0.7 %copy-start.1 = (f32[8,4,128]{2,1,0:T(4,128)S(1)}, f32[8,4,128]{2,1,0:T(4,128)}, u32[]{:S(2)}) copy-start(f32[8,4,128]{2,1,0:T(4,128)} %sus.1) | copy-start | bytes 49156
  2.1 0.7 %copy-start.2 = (s32[2,256]{1,0:T(2,128)S(1)}, s32[2,256]{1,0:T(2,128)}, u32[]{:S(2)}) copy-start(s32[2,256]{1,0:T(2,128)} %cell.1) | copy-start | bytes 6148
  2.8 0.7 %copy-start.3 = (s32[2,256]{1,0:T(2,128)S(1)}, s32[2,256]{1,0:T(2,128)}, u32[]{:S(2)}) copy-start(s32[2,256]{1,0:T(2,128)} %line.1) | copy-start | bytes 6148
  3.4 0.7 %copy-start.4 = (f32[2,256]{1,0:T(2,128)S(1)}, f32[2,256]{1,0:T(2,128)}, u32[]{:S(2)}) copy-start(f32[2,256]{1,0:T(2,128)} %obs.1) | copy-start | bytes 6148
  4.1 0.7 %copy-start.5 = (f32[2,256]{1,0:T(2,128)S(1)}, f32[2,256]{1,0:T(2,128)}, u32[]{:S(2)}) copy-start(f32[2,256]{1,0:T(2,128)} %wgt.1) | copy-start | bytes 6148
  4.8 0.7 %copy-start.6 = (f32[8]{0:T(128)S(1)}, f32[8]{0:T(128)}, u32[]{:S(2)}) copy-start(f32[8]{0:T(128)} %steps.1) | copy-start | bytes 100
